TPU v7x, 32 devices: a whole 2x2x4 slice. The times are simulated.
32 devices in a mesh: ma: 16 (over z, y, core), row: 2 (over x).
Axes of the slice: x: 2, y: 2, z: 4, core: 2. Of those that a mesh axis runs over, the one named last changes fastest.
Arguments:
- spectral: bfloat16 [384, 2, 384, 2, 769], P('ma', None, 'row'), may hold values from -0.011047363 to 0.011047363
- latitude_basis: bfloat16 [384, 769, 1152], P('ma'), may hold values from -0.21875 to 0.21875
- pair_orders: int32 [384], replicated, may hold values from 0 to 383, each once
Outputs:
- grid_values: bfloat16 [64, 2, 1152, 2304], P('row', None, 'ma')
Inputs may be any that keep to these rules, and one draw needn't show every extreme that they name: A permutation of 0 to 383; slot p holds the orders pair_orders[p] and 767 - pair_orders[p].
All inputs are finite; a program needn't handle non-finite values.
Results may differ from a plain program's by a relative error of at most 0.0066.
Values may be sent and summed in bfloat16 or wider, within the bound.
A program may use at most 192 MiB of HBM per device.

v0:
```python
import math

import jax
import jax.numpy as jnp
from jax import lax
from jax.sharding import PartitionSpec as P

NLON = 2304
LEV = 64


def radial_table(total_modes, levels):
    mode_index = lax.broadcasted_iota(jnp.int32, (total_modes, levels), 0)
    points = lax.broadcasted_iota(jnp.int32, (total_modes, levels), 1)
    period = 2 * (total_modes - 1)
    phase_steps = mode_index * points % period
    return jnp.cos(phase_steps.astype(jnp.float32) * (2.0 * math.pi / period)).astype(jnp.bfloat16)


def longitude_table(pair_orders, degrees, points):
    orders = jnp.stack([pair_orders, degrees - 1 - pair_orders], axis=1)
    weights = jnp.where(orders == 0, 1.0, 2.0).astype(jnp.float32)
    phase_index = orders[:, :, None] * lax.broadcasted_iota(jnp.int32, (1, 1, points), 2) % points
    angles = phase_index.astype(jnp.float32) * (2.0 * math.pi / points)
    real_part = weights[:, :, None] * jnp.cos(angles)
    imag_part = -weights[:, :, None] * jnp.sin(angles)
    stacked = jnp.stack([real_part, imag_part], axis=2)
    return stacked.reshape(-1, points).astype(jnp.bfloat16)


def order_selectors(local_orders, degrees, packed):
    packed_rows = lax.broadcasted_iota(jnp.int32, (local_orders.shape[0], packed), 1)
    below_split = packed_rows < (degrees - local_orders)[:, None]
    return jnp.stack([below_split, jnp.logical_not(below_split)], axis=1).astype(jnp.bfloat16)


def per_device(spectral, latitude_basis, pair_orders):
    pair_dev = spectral.shape[0]
    local_modes = spectral.shape[2]
    fields = spectral.shape[3]
    packed = spectral.shape[4]
    degrees = packed - 1
    row_count = lax.axis_size("row")
    total_modes = local_modes * row_count
    level_dev = LEV // row_count
    cheb_table = radial_table(total_modes, LEV)
    own_rows = lax.dynamic_slice_in_dim(
        cheb_table, lax.axis_index("row") * local_modes, local_modes, 0
    )
    scattered = lax.psum_scatter(
        jnp.einsum("pckfr,kl->lpcfr", spectral, own_rows, preferred_element_type=jnp.float32),
        "row",
        scatter_dimension=0,
        tiled=True,
    )
    summed = jnp.transpose(scattered, (1, 2, 0, 3, 4))
    levels = summed.astype(jnp.bfloat16)
    local_orders = lax.dynamic_slice_in_dim(
        pair_orders, lax.axis_index("ma") * pair_dev, pair_dev, 0
    )
    selectors = order_selectors(local_orders, degrees, packed)
    masked = levels[:, None] * selectors[:, :, None, None, None, :]
    lon_table = longitude_table(pair_orders, degrees, NLON)
    block_levels = masked.shape[3]
    fourier = jnp.einsum(
        "phclfr,prt->phclft", masked, latitude_basis, preferred_element_type=jnp.float32
    ).astype(jnp.bfloat16)
    fourier = fourier.reshape(pair_dev * 4, block_levels * fields, fourier.shape[-1])
    synthesized = jnp.einsum(
        "oit,on->itn",
        lax.all_to_all(fourier, "ma", split_axis=2, concat_axis=0, tiled=True),
        lon_table,
        preferred_element_type=jnp.float32,
    ).astype(jnp.bfloat16)
    return synthesized.reshape(level_dev, fields, synthesized.shape[1], synthesized.shape[2])


def solution(mesh):
    return jax.shard_map(
        per_device,
        mesh=mesh,
        in_specs=(P("ma", None, "row", None, None), P("ma", None, None), P()),
        out_specs=P("row", None, "ma", None),
        check_vma=False,
    )
```

profile of v0, /device:TPU:13, one launch (start us, length us, event | category | flops | bytes accessed | tf_op | source)
XLA Modules:
  0.0 924.5 jit_solution(17404826338071164951)
XLA Ops:
  6.5 0.0 reduce-scatter.2.cloned.1.call-start
  6.5 0.1 fusion.15
  6.7 25.3 %fusion.2 = f32[64,24,2,2,769]{4,0,3,2,1:T(8,128)} fusion(bf16[24,2,192,2,769]{4,3,2,1,0:T(2,128)(2,1)} %param.3, s32[384,64]{0,1:T(8,128)S(1)} %multiply_remainder_fusion.1, s32[]{:T(128)S(6)} %select_n.42, pred[384,64]{0,1:T(32,128)(4,1)S(1)} %get-tuple-element.11, pred[384,64]{0,1:T(32,128)(4,1)S(1)} %get-tuple-element.12), kind=kOutput, calls=%fused_computation.2 | convolution fusion | flops 1814372352 | bytes 47345668 | tf_op jit(solution)/shard_map/pckfr,kl->lpcfr/dot_general | solution.py:51
  32.0 0.0 copy-start
  32.0 0.0 reduce-scatter.2.cloned.1.call-update
  32.0 0.7 copy-done
  32.7 0.1 dynamic-slice_subtract_fusion
  32.7 0.2 iota_compare_fusion
  33.0 0.2 add_convert_fusion
  33.2 245.5 %reduce-scatter.2.cloned.1.call-done = f32[32,24,2,2,769]{4,0,3,2,1:T(8,128)} async-done(((f32[64,24,2,2,769]{4,0,3,2,1:T(8,128)}), f32[32,24,2,2,769]{4,0,3,2,1:T(8,128)}) %reduce-scatter.2.cloned.1.call-update) | async-done | bytes 9449488 | tf_op jit(solution)/shard_map/reduce_scatter | solution.py:50
  278.7 7.5 convert_bitcast_fusion
  286.1 51.0 %fusion.4 = bf16[24,2,2,32,2,1152]{5,3,4,2,1,0:T(8,128)(2,1)} fusion(bf16[24,769,1152,1,1,1]{2,0,1,5,4,3:T(8,128)(2,1)} %bitcast.18, bf16[24,2,769]{2,1,0:T(2,128)(2,1)S(1)} %add_convert_fusion, bf16[24,2,32,2,769]{4,2,3,1,0:T(8,128)(2,1)} %convert_bitcast_fusion), kind=kOutput, calls=%fused_computation.5 | convolution fusion | flops 10897594368 | bytes 61476960 | tf_op jit(solution)/shard_map/phclfr,prt->phclft/dot_general | solution.py:65
  337.1 20.9 %copy.38 = bf16[24,2,2,32,2,1152]{5,4,3,2,1,0:T(2,128)(2,1)} copy(bf16[24,2,2,32,2,1152]{5,3,4,2,1,0:T(8,128)(2,1)} %fusion.4) | data formatting | bytes 28311552 | tf_op jit(solution)/shard_map/convert_element_type | solution.py:67
  358.0 29.1 %reshape.152 = bf16[96,64,1152]{2,1,0:T(8,128)(2,1)} reshape(bf16[24,2,2,32,2,1152]{5,4,3,2,1,0:T(2,128)(2,1)} %copy.38) | data formatting | bytes 28311552 | tf_op jit(solution)/shard_map/reshape | solution.py:68
  387.1 25.5 %copy.39 = bf16[96,64,1152]{0,1,2:T(8,128)(2,1)} copy(bf16[96,64,1152]{2,1,0:T(8,128)(2,1)} %reshape.152) | data formatting | bytes 28311552 | tf_op jit(solution)/shard_map/reshape | solution.py:68
  412.6 6.5 all-to-all-start
  419.2 31.0 %multiply_convert_fusion.1 = (bf16[384,2,1,2304]{3,0,2,1:T(8,128)(2,1)S(1)}, bf16[384,2,1,2304]{3,0,2,1:T(8,128)(2,1)S(1)}) fusion(s32[384,2]{0,1:T(2,128)S(1)} %pad_add_fusion, f32[384,2]{0,1:T(2,128)S(1)} %get-tuple-element.7, f32[384,2]{0,1:T(2,128)S(1)} %get-tuple-element.8), kind=kLoop, calls=%fused_computation.12 | loop fusion | flops 23003136 | bytes 7087104 | tf_op jit(solution)/shard_map/convert
  450.2 0.6 pad_maximum_fusion
  450.9 21.2 %copy.42 = bf16[384,2,2,2304]{3,2,1,0:T(2,128)(2,1)} copy(bf16[384,2,2,2304]{3,0,2,1:T(8,128)(2,1)S(1)} %pad_maximum_fusion) | data formatting | bytes 14155776 | tf_op jit(solution)/shard_map/stack | solution.py:27
  472.1 15.2 %reshape.156 = bf16[1536,2304,1]{1,0,2:T(8,128)(2,1)} reshape(bf16[384,2,2,2304]{3,2,1,0:T(2,128)(2,1)} %copy.42) | data formatting | bytes 14155776 | tf_op jit(solution)/shard_map/convert_element_type | solution.py:28
  487.3 338.9 %all-to-all-done = bf16[96,64,1152]{0,1,2:T(8,128)(2,1)} async-done(((bf16[96,64,1152]{0,1,2:T(8,128)(2,1)}), bf16[96,64,1152]{0,1,2:T(8,128)(2,1)}, u32[]{:S(2)}, u32[]{:S(2)}) %all-to-all-start) | async-done | bytes 14155808 | tf_op jit(solution)/shard_map/all_to_all | solution.py:71
  826.2 20.6 %copy.41 = bf16[16,96,64,72]{1,0,3,2:T(8,128)(2,1)} copy(bf16[16,96,64,72]{1,2,3,0:T(8,128)(2,1)} %bitcast.6) | data formatting | bytes 28311552 | tf_op jit(solution)/shard_map/all_to_all | solution.py:71
  846.9 31.2 %all_to_all.16 = bf16[1536,64,72]{0,2,1:T(8,128)(2,1)} reshape(bf16[16,96,64,72]{1,0,3,2:T(8,128)(2,1)} %copy.41) | data formatting | bytes 28311552 | tf_op jit(solution)/shard_map/all_to_all | solution.py:71
  878.1 39.6 %convolution_convert_fusion = bf16[64,72,2304]{2,1,0:T(8,128)(2,1)} fusion(bf16[1536,64,72]{0,2,1:T(8,128)(2,1)} %all_to_all.16, bf16[1536,2304,1]{1,0,2:T(8,128)(2,1)} %reshape.156), kind=kOutput, calls=%fused_computation.4 | convolution fusion | flops 32625524736 | bytes 42467328 | tf_op jit(solution)/shard_map/oit,on->itn/dot_general | solution.py:69
  (6 shorter events, 0.1 us)
Async XLA Ops:
  6.5 272.1 %reduce-scatter.2.cloned.1.call-start = ((), (), s32[]{:S(2)}) async-start(), calls=%async_computation.2 | async-start | bytes 33030144 | tf_op jit(solution)/shard_map/reduce_scatter | solution.py:50
  32.0 0.7 copy-start
  412.6 413.6 %all-to-all-start = ((bf16[96,64,1152]{0,1,2:T(8,128)(2,1)}), bf16[96,64,1152]{0,1,2:T(8,128)(2,1)}, u32[]{:S(2)}, u32[]{:S(2)}) async-start(bf16[96,64,1152]{0,1,2:T(8,128)(2,1)} %copy.39), calls=%async_computation.1 | async-start | bytes 37748736 | tf_op jit(solution)/shard_map/all_to_all | solution.py:71
Sparse Core Ops, SparseCore 0:
  32.1 246.4 reduce-scatter.1
where the time goes:
time: 927 us; the launch traced here: 924 us
  waiting for transfers between devices  584 us (63%)
  local copies, waits for them, and re-layouts  164 us (18%)
  matrix products  116 us (13%)
  other arithmetic  39.8 us (4%)
  between operations  13.5 us (1%)
    all_to_all x1, waiting for transfers between devices, per_device(): lax.all_to_all(fourier, 'ma', split_axis=2, concat_axis=0, tiled=True)  339 us
    reduce_scatter x1, waiting for transfers between devices, per_device(): lax.psum_scatter(jnp.einsum('pckfr,kl->lpcfr', spectral, own_rows, prefer...  245 us
    reshape x2, local copies, waits for them, and re-layouts, per_device(): fourier.reshape(pair_dev * 4, block_levels * fields, fourier.shape[-1])  54.6 us
    all_to_all x2, local copies, waits for them, and re-layouts, per_device(): lax.all_to_all(fourier, 'ma', split_axis=2, concat_axis=0, tiled=True)  51.9 us
    dot_general x1, matrix products, per_device(): jnp.einsum('phclfr,prt->phclft', masked, latitude_basis, preferred_elemen...  51 us
    dot_general x1, matrix products, per_device(): jnp.einsum('oit,on->itn', lax.all_to_all(fourier, 'ma', split_axis=2, con...  39.6 us
    another operation x1, other arithmetic  31 us
    dot_general x1, matrix products, per_device(): jnp.einsum('pckfr,kl->lpcfr', spectral, own_rows, preferred_element_type=...  25.3 us
  transfers between devices with their start and end apart: 2, of which 2 were waited for; matrix products, arithmetic and copies ran while one was open for 7% of the time, Pallas kernels for 0%

commit v1 on v0

v1 whole, which is shorter than its diff:
```python
import functools
import math

import jax
import jax.numpy as jnp
from jax import lax
from jax.experimental import pallas as pl
from jax.experimental.pallas import tpu as pltpu
from jax.sharding import PartitionSpec as P

NLON = 2304
LEV = 64
CHUNKS = 2
TILE = 24


def radial_table(total_modes, levels):
    mode_index = lax.broadcasted_iota(jnp.int32, (total_modes, levels), 0)
    points = lax.broadcasted_iota(jnp.int32, (total_modes, levels), 1)
    period = 2 * (total_modes - 1)
    phase_steps = mode_index * points % period
    return jnp.cos(phase_steps.astype(jnp.float32) * (2.0 * math.pi / period)).astype(jnp.bfloat16)


def longitude_table(pair_orders, degrees, points):
    orders = jnp.stack([pair_orders, degrees - 1 - pair_orders], axis=0)
    weights = jnp.where(orders == 0, 1.0, 2.0).astype(jnp.float32)
    phase_index = orders[:, :, None] * lax.broadcasted_iota(jnp.int32, (1, 1, points), 2) % points
    angles = phase_index.astype(jnp.float32) * (2.0 * math.pi / points)
    real_part = weights[:, :, None] * jnp.cos(angles)
    imag_part = -weights[:, :, None] * jnp.sin(angles)
    stacked = jnp.stack([real_part.astype(jnp.bfloat16), imag_part.astype(jnp.bfloat16)], axis=1)
    return stacked.reshape(-1, points)


def order_selectors(local_orders, degrees, packed):
    packed_rows = lax.broadcasted_iota(jnp.int32, (local_orders.shape[0], packed), 1)
    below_split = packed_rows < (degrees - local_orders)[:, None]
    return jnp.stack([below_split, jnp.logical_not(below_split)], axis=1).astype(jnp.bfloat16)


def synth_kernel(subs, tile, *refs):
    count = piece_count(subs)
    pieces, table_ref, out_ref, rows_ref = refs[:count], refs[count], refs[-2], refs[-1]
    images = out_ref.shape[0]
    points = out_ref.shape[2]

    def gather(t, carry):
        slot = 0
        for piece, start, size in subs:
            block = pieces[piece][:, t]
            block = block[:, start : start + size].astype(jnp.float32)
            turned = block.reshape(-1, block.shape[-1]).T
            for part in range(turned.shape[0] // images):
                for lane in range(turned.shape[1] // 128):
                    rows_ref[slot, pl.ds(t, images, stride=tile), :] = turned[
                        part * images : (part + 1) * images, lane * 128 : (lane + 1) * 128
                    ]
                    slot += 1
        return carry

    lax.fori_loop(0, tile, gather, 0)
    rows = jnp.concatenate(
        [rows_ref[slot].astype(jnp.bfloat16) for slot in range(rows_ref.shape[0])], axis=1
    )
    width = points // 3
    for cut in range(3):
        cols = slice(cut * width, (cut + 1) * width)
        sums = jnp.dot(rows, table_ref[:, cols], preferred_element_type=jnp.float32)
        out_ref[:, :, cols] = sums.reshape(images, tile, width).astype(jnp.bfloat16)


def piece_count(subs):
    return 1 + max(piece for piece, _, _ in subs)


def synthesize(pieces, subs, table, whole, images, chunk, total):
    lats, lanes = pieces[0].shape[1], pieces[0].shape[3]
    points = table.shape[1]
    tile = TILE
    in_specs = [
        pl.BlockSpec((p.shape[0], tile, p.shape[2], lanes), lambda t: (0, t, 0, 0)) for p in pieces
    ]
    in_specs.append(pl.BlockSpec(table.shape, lambda t: (0, 0)))
    operands = list(pieces) + [table]
    aliases = {}
    if whole is not None:
        in_specs.append(pl.BlockSpec(memory_space=pl.ANY))
        aliases = {len(operands): 0}
        operands.append(whole)
    return pl.pallas_call(
        functools.partial(synth_kernel, tuple(subs), tile),
        grid=(lats // tile,),
        in_specs=in_specs,
        out_specs=pl.BlockSpec((images, tile, points), lambda t: (chunk, t, 0)),
        out_shape=jax.ShapeDtypeStruct((total, lats, points), jnp.bfloat16),
        scratch_shapes=[pltpu.VMEM((table.shape[0] // 128, images * tile, 128), jnp.float32)],
        input_output_aliases=aliases,
        compiler_params=pltpu.CompilerParams(vmem_limit_bytes=60 * 1024 * 1024),
        cost_estimate=pl.CostEstimate(
            flops=2 * images * lats * points * table.shape[0],
            bytes_accessed=2 * (images * lats * (points + table.shape[0]) + table.size),
            transcendentals=0,
        ),
        name="synthesize",
    )(*operands)


def per_device(spectral, latitude_basis, pair_orders):
    pair_dev, parts, local_modes, fields, packed = spectral.shape
    degrees = packed - 1
    row_count = lax.axis_size("row")
    ma_count = lax.axis_size("ma")
    lats = latitude_basis.shape[2]
    own_lats = lats // ma_count
    row = lax.axis_index("row")
    total_modes = local_modes * row_count
    level_dev = LEV // row_count
    step = level_dev // CHUNKS
    lanes = 2 * parts * step * fields
    fused = own_lats % TILE == 0 and pair_dev % 8 == 0 and lanes == 128 and ma_count % 16 == 0
    if fused and pair_dev > 8:
        splits = [[(0, 8), (8, pair_dev)]] + [[(0, pair_dev)]] * (CHUNKS - 1)
        groups = [(0, 8), (8, pair_dev)]
    else:
        splits = [[(0, pair_dev)]] * CHUNKS
        groups = [(0, pair_dev)]
    cheb_table = radial_table(total_modes, LEV)
    own_rows = lax.dynamic_slice_in_dim(cheb_table, row * local_modes, local_modes, 0)
    local_orders = lax.dynamic_slice_in_dim(
        pair_orders, lax.axis_index("ma") * pair_dev, pair_dev, 0
    )
    selectors = order_selectors(local_orders, degrees, packed)
    by_owner = pair_orders.reshape(ma_count, pair_dev)
    lon_table = jnp.concatenate(
        [longitude_table(by_owner[:, a:b].reshape(-1), degrees, NLON) for a, b in groups], axis=0
    )

    def partial(owner, chunk):
        table = lax.dynamic_slice_in_dim(own_rows, owner * level_dev + chunk * step, step, 1)
        return jnp.einsum("pckfr,kl->pclfr", spectral, table, preferred_element_type=jnp.float32)

    def received(chunk):
        hops = []
        for hop in range(1, row_count):
            away = partial((row + hop) % row_count, chunk).astype(jnp.bfloat16)
            ring = [(i, (i + hop) % row_count) for i in range(row_count)]
            parts_of = []
            for a, b in splits[chunk]:
                parts_of.append(lax.ppermute(away[a:b], "row", ring))
            hops.append(parts_of)
        return hops

    whole, outs = None, []
    for chunk in range(CHUNKS):
        hops = received(chunk)
        own = partial(row, chunk)
        pieces = []
        for part, (a, b) in enumerate(splits[chunk]):
            total = own[a:b]
            for hop in hops:
                total = total + hop[part].astype(jnp.float32)
            levels = total.astype(jnp.bfloat16)
            own_selectors, levels = lax.optimization_barrier((selectors[a:b], levels))
            masked = levels[:, None] * own_selectors[:, :, None, None, None, :]
            masked = masked.reshape(b - a, lanes, packed)
            fourier = jnp.einsum(
                "prt,pmr->tpm", latitude_basis[a:b], masked, preferred_element_type=jnp.float32
            ).astype(jnp.bfloat16)
            got = lax.all_to_all(fourier, "ma", split_axis=0, concat_axis=0, tiled=True)
            pieces.append(got.reshape(ma_count, own_lats, b - a, lanes))
        if fused:
            if len(pieces) > 1:
                subs = [(n, 0, b - a) for n, (a, b) in enumerate(groups)]
            else:
                subs = [(0, a, b - a) for a, b in groups]
            whole = synthesize(
                pieces, subs, lon_table, whole, step * fields, chunk, level_dev * fields
            )
        else:
            got = pieces[0].reshape(ma_count, own_lats, pair_dev, 2 * parts, step * fields)
            got = jnp.transpose(got, (4, 1, 3, 0, 2)).reshape(step * fields, own_lats, -1)
            synthesized = jnp.einsum(
                "ito,on->itn", got, lon_table, preferred_element_type=jnp.float32
            ).astype(jnp.bfloat16)
            outs.append(synthesized)
    if not fused:
        whole = jnp.concatenate(outs, axis=0)
    return whole.reshape(level_dev, fields, own_lats, NLON)


def solution(mesh):
    return jax.shard_map(
        per_device,
        mesh=mesh,
        in_specs=(P("ma", None, "row", None, None), P("ma", None, None), P()),
        out_specs=P("row", None, "ma", None),
        check_vma=False,
    )
```

time: 927 us -> 511 us (0.55)
  waiting for transfers between devices: 584 us -> 189 us
  local copies, waits for them, and re-layouts: 164 us -> 57.2 us
  Pallas kernels: 0 us -> 62.3 us
  starting transfers between devices: 6.54 us -> 23 us
  between operations: 13.5 us -> 0.49 us
    all_to_all x1 -> x3, waiting for transfers between devices: 339 us -> 87.2 us  [per_device(): got = lax.all_to_all(fourier, 'ma', split_axis=0, concat_axis=0, tiled=True)]
    reduce_scatter x1 -> x0, waiting for transfers between devices: 245 us -> none  [per_device(): lax.psum_scatter(jnp.einsum('pckfr,kl->lpcfr', spectral, own_rows, prefer...]
    ppermute x0 -> x3, waiting for transfers between devices: none -> 102 us  [received(): parts_of.append(lax.ppermute(away[a:b], 'row', ring))]
    pallas_call x0 -> x2, Pallas kernels: none -> 62.3 us  [synthesize(): pl.pallas_call(functools.partial(synth_kernel, tuple(subs), tile), grid=(...]
    reshape x2 -> x1, local copies, waits for them, and re-layouts: 54.6 us -> 0.08 us  [per_device(): by_owner = pair_orders.reshape(ma_count, pair_dev)]
    all_to_all x2 -> x0, local copies, waits for them, and re-layouts: 51.9 us -> none  [per_device(): lax.all_to_all(fourier, 'ma', split_axis=2, concat_axis=0, tiled=True)]
    another operation x3 -> x4, other arithmetic: 31.7 us -> 0.67 us  [the longest x2 0.65 us: longitude_table(): jnp.stack([real_part.astype(jnp.bfloat16), imag_part.astype(jnp.bfloat16)...]
    convert_element_type x1 -> x5, other arithmetic: 7.46 us -> 36.4 us  [the longest x2 31.5 us: longitude_table(): real_part.astype(jnp.bfloat16)]
  transfers between devices with their start and end apart: 2 -> 6, of which waited for: 2 -> 3; matrix products, arithmetic and copies ran while one was open for 7% -> 38% of each run, Pallas kernels for 0% -> 6%
where the time goes in v1:
time: 511 us; the launch traced here: 502 us
  waiting for transfers between devices  189 us (37%)
  matrix products  124 us (24%)
  Pallas kernels  62.3 us (12%)
  local copies, waits for them, and re-layouts  57.2 us (11%)
  other arithmetic  45.8 us (9%)
  starting transfers between devices  23 us (5%)
    ppermute x3, waiting for transfers between devices, received(): parts_of.append(lax.ppermute(away[a:b], 'row', ring))  102 us
    all_to_all x3, waiting for transfers between devices, per_device(): got = lax.all_to_all(fourier, 'ma', split_axis=0, concat_axis=0, tiled=True)  87.2 us
    dot_general x4, matrix products, partial(): jnp.einsum('pckfr,kl->pclfr', spectral, table, preferred_element_type=jnp...  67.9 us
    pallas_call x2, Pallas kernels, synthesize(): pl.pallas_call(functools.partial(synth_kernel, tuple(subs), tile), grid=(...  62.3 us
    dot_general x3, matrix products, per_device(): jnp.einsum('prt,pmr->tpm', latitude_basis[a:b], masked, preferred_element...  56.1 us
    convert_element_type x2, other arithmetic, longitude_table(): real_part.astype(jnp.bfloat16)  31.5 us
    unnamed x7, local copies, waits for them, and re-layouts  29 us
    convert_element_type x3, local copies, waits for them, and re-layouts, per_device(): fourier = jnp.einsum('prt,pmr->tpm', latitude_basis[a:b], masked, preferr...  22.3 us
  transfers between devices with their start and end apart: 6, of which 3 were waited for; matrix products, arithmetic and copies ran while one was open for 38% of the time, Pallas kernels for 6%

profile of v1, /device:TPU:13, one launch (start us, length us, event | category | flops | bytes accessed | tf_op | source)
XLA Modules:
  0.0 501.8 jit_solution(6878747768818150718)
XLA Ops:
  0.0 0.4 fusion.52
  0.4 16.4 %convert_bitcast_fusion.1 = bf16[24,2,16,2,769]{4,2,3,1,0:T(8,128)(2,1)S(1)} fusion(bf16[24,2,192,2,769]{4,3,2,1,0:T(2,128)(2,1)} %param.3, bf16[384,64]{0,1:T(8,128)(2,1)S(1)} %fusion.52, s32[]{:T(128)S(6)} %select_n.108, s32[]{:T(128)S(6)} %select_n.121), kind=kOutput, calls=%fused_computation.35 | convolution fusion | flops 454755840 | bytes 30718984 | tf_op jit(solution)/shard_map/pckfr,kl->pclfr/dot_general | solution.py:141
  16.8 1.1 slice.44
  17.9 1.2 collective-permute-start.1
  19.1 17.9 %fusion.35 = f32[24,2,16,2,769]{4,2,3,1,0:T(8,128)} fusion(bf16[24,2,192,2,769]{4,3,2,1,0:T(2,128)(2,1)} %param.3, bf16[384,64]{0,1:T(8,128)(2,1)S(1)} %fusion.52, s32[]{:T(128)S(6)} %select_n.108, s32[]{:T(128)S(6)} %select_n.119), kind=kOutput, calls=%fused_computation.38 | convolution fusion | flops 453574656 | bytes 33081352 | tf_op jit(solution)/shard_map/pckfr,kl->pclfr/dot_general | solution.py:141
  37.0 28.9 %copy.38 = bf16[24,769,1152]{2,1,0:T(8,128)(2,1)} copy(bf16[24,769,1152]{2,0,1:T(8,128)(2,1)} %param.4) | data formatting | bytes 85045248 | tf_op args[1]
  66.0 0.1 dynamic-slice_subtract_fusion
  66.1 0.1 iota_compare_fusion
  66.2 0.0 collective-permute-done.1
  66.2 2.0 fusion.47
  68.2 0.5 copy.42
  68.7 0.2 broadcast_multiply_fusion.2
  68.9 9.4 %fusion.30 = bf16[1152,8,128]{0,2,1:T(8,128)(2,1)} fusion(bf16[24,769,1152]{2,1,0:T(8,128)(2,1)} %copy.38, bf16[8,128,769]{2,0,1:T(8,128)(2,1)S(1)} %bitcast.50), kind=kOutput, calls=%fused_computation.34 | convolution fusion | flops 1815478272 | bytes 18237440 | tf_op jit(solution)/shard_map/prt,pmr->tpm/dot_general | solution.py:167
  78.3 4.5 copy.45
  82.8 6.8 %all-to-all-start.1 = ((bf16[1152,8,128]{2,1,0:T(8,128)(2,1)}), bf16[1152,8,128]{2,1,0:T(8,128)(2,1)}, u32[]{:S(2)}, u32[]{:S(2)}) async-start(bf16[1152,8,128]{2,1,0:T(8,128)(2,1)} %copy.45), calls=%async_computation.1 | async-start | bytes 4718592 | tf_op jit(solution)/shard_map/all_to_all | solution.py:170
  89.6 1.4 slice.48
  91.0 0.2 collective-permute-start.2
  91.3 0.0 copy-done
  91.3 41.1 %collective-permute-done.2 = bf16[16,2,16,2,769]{4,2,3,1,0:T(8,128)(2,1)S(1)} collective-permute-done((bf16[16,2,16,2,769]{4,2,3,1,0:T(8,128)(2,1)}, bf16[16,2,16,2,769]{4,2,3,1,0:T(8,128)(2,1)S(1)}, u32[]{:S(2)}, u32[]{:S(2)}) %collective-permute-start.2) | collective-permute-done | bytes 1574944 | tf_op jit(solution)/shard_map/ppermute | solution.py:150
  132.4 2.6 fusion.28
  135.0 1.0 copy.46
  136.0 2.2 broadcast_multiply_fusion.1
  138.2 15.4 %fusion.22 = bf16[1152,16,128]{0,2,1:T(8,128)(2,1)} fusion(bf16[24,769,1152]{2,1,0:T(8,128)(2,1)} %copy.38, bf16[16,128,769]{2,0,1:T(8,128)(2,1)} %bitcast.49), kind=kOutput, calls=%fused_computation.28 | convolution fusion | flops 3630956544 | bytes 36995072 | tf_op jit(solution)/shard_map/prt,pmr->tpm/dot_general | solution.py:167
  153.6 7.1 %copy.49 = bf16[1152,16,128]{2,1,0:T(8,128)(2,1)} copy(bf16[1152,16,128]{0,2,1:T(8,128)(2,1)} %fusion.22) | data formatting | bytes 9437184 | tf_op jit(solution)/shard_map/convert_element_type | solution.py:169
  160.7 0.0 all-to-all-done.1
  160.7 7.2 %all-to-all-start.2 = ((bf16[1152,16,128]{2,1,0:T(8,128)(2,1)}), bf16[1152,16,128]{2,1,0:T(8,128)(2,1)}, u32[]{:S(2)}, u32[]{:S(2)}) async-start(bf16[1152,16,128]{2,1,0:T(8,128)(2,1)} %copy.49), calls=%async_computation.2 | async-start | bytes 9437184 | tf_op jit(solution)/shard_map/all_to_all | solution.py:170
  167.9 16.4 %convert_bitcast_fusion.2 = bf16[24,2,16,2,769]{4,2,3,1,0:T(8,128)(2,1)S(1)} fusion(bf16[24,2,192,2,769]{4,3,2,1,0:T(2,128)(2,1)} %param.3, bf16[384,64]{0,1:T(8,128)(2,1)S(1)} %fusion.52, s32[]{:T(128)S(6)} %select_n.108, s32[]{:T(128)S(6)} %select_n.113), kind=kOutput, calls=%fused_computation.37 | convolution fusion | flops 454755840 | bytes 30718984 | tf_op jit(solution)/shard_map/pckfr,kl->pclfr/dot_general | solution.py:141
  184.4 0.3 collective-permute-start
  184.7 60.7 %collective-permute-done = bf16[24,2,16,2,769]{4,2,3,1,0:T(8,128)(2,1)} collective-permute-done((bf16[24,2,16,2,769]{4,2,3,1,0:T(8,128)(2,1)S(1)}, bf16[24,2,16,2,769]{4,2,3,1,0:T(8,128)(2,1)}, u32[]{:S(2)}, u32[]{:S(2)}) %collective-permute-start) | collective-permute-done | bytes 2362400 | tf_op jit(solution)/shard_map/ppermute | solution.py:150
  245.4 17.2 %fusion.12 = bf16[24,2,16,2,769]{4,2,3,1,0:T(8,128)(2,1)S(1)} fusion(bf16[24,2,16,2,769]{4,2,3,1,0:T(8,128)(2,1)} %collective-permute-done, bf16[24,2,192,2,769]{4,3,2,1,0:T(2,128)(2,1)} %param.3, bf16[384,64]{0,1:T(8,128)(2,1)S(1)} %fusion.52, s32[]{:T(128)S(6)} %select_n.108, s32[]{:T(128)S(6)} %select_n.110), kind=kOutput, calls=%fused_computation.16 | convolution fusion | flops 457118208 | bytes 33081352 | tf_op jit(solution)/shard_map/pckfr,kl->pclfr/dot_general | solution.py:141
  262.6 1.5 copy.36
  264.1 2.9 broadcast_multiply_fusion
  267.0 31.3 %convert_bitcast_fusion = bf16[1152,24,128]{0,2,1:T(8,128)(2,1)} fusion(bf16[24,128,769]{2,0,1:T(8,128)(2,1)} %bitcast.48, bf16[24,769,1152]{2,0,1:T(8,128)(2,1)} %param.4), kind=kOutput, calls=%fused_computation.13 | convolution fusion | flops 5446434816 | bytes 54325248 | tf_op jit(solution)/shard_map/prt,pmr->tpm/dot_general | solution.py:167
  298.4 10.7 %copy.39 = bf16[1152,24,128]{2,1,0:T(8,128)(2,1)} copy(bf16[1152,24,128]{0,2,1:T(8,128)(2,1)} %convert_bitcast_fusion) | data formatting | bytes 14155776 | tf_op jit(solution)/shard_map/convert_element_type | solution.py:169
  309.0 0.0 all-to-all-done.2
  309.1 7.2 %all-to-all-start = ((bf16[1152,24,128]{2,1,0:T(8,128)(2,1)}), bf16[1152,24,128]{2,1,0:T(8,128)(2,1)}, u32[]{:S(2)}, u32[]{:S(2)}) async-start(bf16[1152,24,128]{2,1,0:T(8,128)(2,1)} %copy.39), calls=%async_computation | async-start | bytes 14155776 | tf_op jit(solution)/shard_map/all_to_all | solution.py:170
  316.3 0.1 reshape.263
  316.4 0.1 slice.41
  316.4 0.1 stack.31
  316.5 0.1 stack.28
  316.7 10.4 %multiply_convert_fusion.3 = (bf16[2,1,128,2304]{3,2,1,0:T(8,128)(2,1)S(1)}, bf16[2,1,128,2304]{3,2,1,0:T(8,128)(2,1)S(1)}) fusion(s32[2,128]{1,0:T(2,128)S(1)} %pad_add_fusion.1, f32[2,128]{1,0:T(2,128)S(1)} %get-tuple-element.23, f32[2,128]{1,0:T(2,128)S(1)} %get-tuple-element.24), kind=kLoop, calls=%fused_computation.43 | loop fusion | flops 7667712 | bytes 2362368 | tf_op jit(solution)/shard_map/convert_element_type | solution.py:32
  327.1 0.2 pad_maximum_fusion.2
  327.4 21.0 %multiply_convert_fusion.1 = (bf16[2,1,256,2304]{3,2,1,0:T(8,128)(2,1)S(1)}, bf16[2,1,256,2304]{3,2,1,0:T(8,128)(2,1)S(1)}) fusion(s32[2,256]{1,0:T(2,128)S(1)} %pad_add_fusion, f32[2,256]{1,0:T(2,128)S(1)} %get-tuple-element.19, f32[2,256]{1,0:T(2,128)S(1)} %get-tuple-element.20), kind=kLoop, calls=%fused_computation.23 | loop fusion | flops 15335424 | bytes 4724736 | tf_op jit(solution)/shard_map/convert_element_type | solution.py:32
  348.4 0.4 pad_maximum_fusion.1
  348.8 3.3 pad_maximum_fusion.refs_2_.refs_1_
  352.1 31.1 %synthesize.2.refs_2_ = bf16[64,72,2304]{2,1,0:T(8,128)(2,1)} custom-call(bf16[16,72,8,128]{3,2,1,0:T(8,128)(2,1)} %bitcast.19.refs_0_, bf16[16,72,16,128]{3,2,1,0:T(8,128)(2,1)} %bitcast.22.refs_1_, bf16[1536,2304]{1,0:T(8,128)(2,1)} %pad_maximum_fusion.refs_2_.refs_1_), custom_call_target="tpu_custom_call" | custom-call | flops 16307453952 | bytes 24772608 | tf_op jit(solution)/shard_map/synthesize/pallas_call | solution.py:91
  383.2 87.2 %all-to-all-done = bf16[1152,24,128]{2,1,0:T(8,128)(2,1)} async-done(((bf16[1152,24,128]{2,1,0:T(8,128)(2,1)}), bf16[1152,24,128]{2,1,0:T(8,128)(2,1)}, u32[]{:S(2)}, u32[]{:S(2)}) %all-to-all-start) | async-done | bytes 7077920 | tf_op jit(solution)/shard_map/all_to_all | solution.py:170
  470.4 31.2 %synthesize.3 = bf16[64,72,2304]{2,1,0:T(8,128)(2,1)} custom-call(bf16[16,72,24,128]{3,2,1,0:T(8,128)(2,1)} %bitcast.8.refs_0_, bf16[1536,2304]{1,0:T(8,128)(2,1)} %pad_maximum_fusion.refs_2_.refs_1_, bf16[64,72,2304]{2,1,0:T(8,128)(2,1)} %synthesize.2.refs_2_), custom_call_target="tpu_custom_call", output_to_operand_aliasing={{}: (2, {})} | custom-call | flops 16307453952 | bytes 24772608 | tf_op jit(solution)/shard_map/synthesize/pallas_call | solution.py:91
  (15 shorter events, 0.1 us)
Async XLA Ops:
  17.9 48.3 %collective-permute-start.1 = (bf16[8,2,16,2,769]{4,2,3,1,0:T(8,128)(2,1)}, bf16[8,2,16,2,769]{4,2,3,1,0:T(8,128)(2,1)}, u32[]{:S(2)}, u32[]{:S(2)}) collective-permute-start(bf16[8,2,16,2,769]{4,2,3,1,0:T(8,128)(2,1)} %slice.44), channel_id=1, source_target_pairs={{0,1},{1,0},{2,3},{3,2},{4,5},{5,4},{6,7},{7,6},{8,9},{9,8},{10,11... | collective-permute-start | bytes 2362376 | tf_op jit(solution)/shard_map/ppermute | solution.py:150
  37.0 29.0 %copy-start.2 = (s32[384]{0:T(512)S(1)}, s32[384]{0:T(512)}, u32[]{:S(2)}) copy-start(s32[384]{0:T(512)} %param.5) | copy-start | bytes 4612
  66.2 25.1 %copy-start = (bf16[24,2,769]{2,0,1:T(8,128)(2,1)}, bf16[24,2,769]{2,0,1:T(8,128)(2,1)S(1)}, u32[]{:S(2)}) copy-start(bf16[24,2,769]{2,0,1:T(8,128)(2,1)S(1)} %add_convert_fusion) | copy-start | bytes 221476
  82.8 77.9 %all-to-all-start.1 = ((bf16[1152,8,128]{2,1,0:T(8,128)(2,1)}), bf16[1152,8,128]{2,1,0:T(8,128)(2,1)}, u32[]{:S(2)}, u32[]{:S(2)}) async-start(bf16[1152,8,128]{2,1,0:T(8,128)(2,1)} %copy.45), calls=%async_computation.1 | async-start | bytes 4718592 | tf_op jit(solution)/shard_map/all_to_all | solution.py:170
  91.0 41.4 %collective-permute-start.2 = (bf16[16,2,16,2,769]{4,2,3,1,0:T(8,128)(2,1)}, bf16[16,2,16,2,769]{4,2,3,1,0:T(8,128)(2,1)S(1)}, u32[]{:S(2)}, u32[]{:S(2)}) collective-permute-start(bf16[16,2,16,2,769]{4,2,3,1,0:T(8,128)(2,1)} %slice.48), channel_id=1, source_target_pairs={{0,1},{1,0},{2,3},{3,2},{4,5},{5,4},{6,7},{7,6},{8,9},{9,8},{10,11... | collective-permute-start | bytes 4724744 | tf_op jit(solution)/shard_map/ppermute | solution.py:150
  91.3 44.7 %slice-start = ((bf16[24,2,769]{2,0,1:T(8,128)(2,1)}), bf16[16,2,769]{2,0,1:T(8,128)(2,1)S(1)}, s32[]{:S(2)}) async-start(bf16[24,2,769]{2,0,1:T(8,128)(2,1)} %copy-done), calls=%async_computation.3 | async-start | bytes 114688 | tf_op jit(solution)/shard_map/slice | solution.py:164
  160.7 148.3 %all-to-all-start.2 = ((bf16[1152,16,128]{2,1,0:T(8,128)(2,1)}), bf16[1152,16,128]{2,1,0:T(8,128)(2,1)}, u32[]{:S(2)}, u32[]{:S(2)}) async-start(bf16[1152,16,128]{2,1,0:T(8,128)(2,1)} %copy.49), calls=%async_computation.2 | async-start | bytes 9437184 | tf_op jit(solution)/shard_map/all_to_all | solution.py:170
  184.4 61.0 %collective-permute-start = (bf16[24,2,16,2,769]{4,2,3,1,0:T(8,128)(2,1)S(1)}, bf16[24,2,16,2,769]{4,2,3,1,0:T(8,128)(2,1)}, u32[]{:S(2)}, u32[]{:S(2)}) collective-permute-start(bf16[24,2,16,2,769]{4,2,3,1,0:T(8,128)(2,1)S(1)} %convert_bitcast_fusion.2), channel_id=1, source_target_pairs={{0,1},{1,0},{2,3},{3,2},{4,5},{5,4},{6,7},{7,6},{8,9},{9,8},{10,11... | collective-permute-start | bytes 7087112 | tf_op jit(solution)/shard_map/ppermute | solution.py:150
  262.5 1.6 copy-start.1
  309.1 161.3 %all-to-all-start = ((bf16[1152,24,128]{2,1,0:T(8,128)(2,1)}), bf16[1152,24,128]{2,1,0:T(8,128)(2,1)}, u32[]{:S(2)}, u32[]{:S(2)}) async-start(bf16[1152,24,128]{2,1,0:T(8,128)(2,1)} %copy.39), calls=%async_computation | async-start | bytes 14155776 | tf_op jit(solution)/shard_map/all_to_all | solution.py:170
